TPU v7x, 512 devices: a whole 4x8x8 slice. The times are simulated.
512 devices in a mesh: tp: 8 (over y), row: 8 (over z_hi, x), col: 8 (over z_lo, core).
Axes of the slice: x: 4, y: 8, z: 8 (z_hi: 2, z_lo: 4; z = z_hi * 4 + z_lo), core: 2. Of those that a mesh axis runs over, the one named last changes fastest.
Arguments:
- hidden: bfloat16 [128, 14336], P('col', 'row'), may hold values from -6 to 6
- out_grad: bfloat16 [128, 4096], P(None, ('tp', 'row')), may hold values from -6 to 6
- basis_in: bfloat16 [14336, 4096], P(('row', 'col'), 'tp'), may hold values from -0.046875 to 0.046875
- basis_out: bfloat16 [4096, 1024], P(('tp', 'row'), 'col'), may hold values from -0.09375 to 0.09375
- eigen: float32 [4096, 1024], P(('tp', 'row'), 'col'), may hold values from 0.02 to 2
Outputs:
- precond: float32 [4096, 14336], P(('tp', 'col'), 'row')
All inputs are finite; a program needn't handle non-finite values.
Results may differ from a plain program's by a relative error of at most 0.024.
Values may be sent and summed in bfloat16 or wider, within the bound.
A program may use at most 64 MiB of HBM per device.

v0:
```python
import jax
import jax.numpy as jnp
from jax import lax
from jax.sharding import PartitionSpec as P

damping = 0.01


def sent_to_all(array, axis):
    devices = lax.axis_size(axis)
    return lax.all_to_all(
        jnp.broadcast_to(array[None], (devices, *array.shape)), axis, 0, 0, tiled=True
    )


def laid_out(tiles, dim):
    dims = list(tiles.shape[1:])
    dims[dim] *= tiles.shape[0]
    return jnp.moveaxis(tiles, 0, dim).reshape(dims)


def gathered_copies(array, axis, dim):
    tiles = sent_to_all(array, axis)
    return laid_out(tiles, dim)


def in_blocks(array, dim, devices):
    before, after = (array.shape[:dim], array.shape[dim + 1 :])
    return jnp.moveaxis(array.reshape(*before, devices, -1, *after), dim, 0)


def sent_and_summed(array, axis, dim):
    tiles = in_blocks(array, dim, lax.axis_size(axis))
    arrived = lax.all_to_all(tiles, axis, split_axis=0, concat_axis=0, tiled=True)
    return arrived.astype(jnp.float32).sum(axis=0)


def contract_rows(left, right):
    return lax.dot_general(
        left, right, (((0,), (0,)), ((), ())), preferred_element_type=jnp.float32
    )


def contract_cols(left, right):
    return lax.dot_general(
        left, right, (((1,), (1,)), ((), ())), preferred_element_type=jnp.float32
    )


def shards(hidden, out_grad, basis_in, basis_out, eigen):
    tp_count = lax.axis_size("tp")
    col_count = lax.axis_size("col")
    basis_block = gathered_copies(basis_in, "col", 0)
    partial_in = jnp.dot(hidden, basis_block, preferred_element_type=jnp.float32)
    rotated_in = sent_and_summed(partial_in.astype(jnp.bfloat16), "row", 1).astype(jnp.bfloat16)
    rotated_in = gathered_copies(rotated_in, "col", 0)
    queries = rotated_in.shape[0]
    out_rows = gathered_copies(basis_out, ("tp", "row"), 0)
    grad_full = lax.all_gather(out_grad, ("tp", "row"), axis=1, tiled=True)
    rotated_out = jnp.dot(grad_full, out_rows, preferred_element_type=jnp.float32).astype(
        jnp.bfloat16
    )
    coeff = contract_rows(rotated_in, rotated_out)
    scaled = (coeff / (queries * (eigen + damping))).astype(jnp.bfloat16)
    mixed_part = contract_cols(scaled, out_rows)
    depth = mixed_part.shape[0]
    width = mixed_part.shape[1]
    mixed_part = mixed_part.reshape(depth, tp_count, col_count, width // (tp_count * col_count))
    mixed = sent_and_summed(mixed_part.astype(jnp.bfloat16), "col", 2)
    mixed = mixed.reshape(depth, width // col_count).astype(jnp.bfloat16)
    mixed = gathered_copies(mixed, "row", 0)
    return sent_and_summed(
        lax.dot_general(
            mixed, basis_block, (((0,), (1,)), ((), ())), preferred_element_type=jnp.float32
        ).astype(jnp.bfloat16),
        "tp",
        0,
    )


def solution(mesh):
    placed = (
        P("col", "row"),
        P(None, ("tp", "row")),
        P(("row", "col"), "tp"),
        P(("tp", "row"), "col"),
        P(("tp", "row"), "col"),
    )
    return jax.shard_map(
        shards, mesh=mesh, in_specs=placed, out_specs=P(("tp", "col"), "row"), check_vma=False
    )
```

profile of v0, /device:TPU:8, one launch (start us, length us, event | category | flops | bytes accessed | tf_op | source)
XLA Modules:
  0.0 334.7 jit_solution(7538081881652696159)
XLA Ops:
  6.5 0.0 copy-start
  6.5 1.1 broadcast_in_dim.8
  7.6 50.5 %all_to_all.35 = bf16[8,224,512]{2,1,0:T(8,128)(2,1)S(1)} all-to-all(bf16[8,224,512]{2,1,0:T(8,128)(2,1)S(1)} %broadcast_in_dim.8), channel_id=1, replica_groups=mesh['tp'=8,'row'=8,'col'=8] {'col'}, dimensions={0} | all-to-all | bytes 3670016 | tf_op jit(solution)/shard_map/all_to_all | solution.py:11
  58.1 0.0 copy-start.2
  58.1 0.0 copy-done
  58.1 0.3 convolution_convert_fusion.3
  58.5 0.0 copy-start.1
  58.5 0.1 reshape.37
  58.6 0.1 reshape.44
  58.7 20.0 %all_to_all.36 = bf16[8,2,512]{2,1,0:T(2,128)(2,1)S(1)} all-to-all(bf16[8,2,512]{2,1,0:T(2,128)(2,1)S(1)} %reshape.44), channel_id=1, replica_groups=mesh['tp'=8,'row'=8,'col'=8] {'row'}, dimensions={0} | all-to-all | bytes 32768 | tf_op jit(solution)/shard_map/all_to_all | solution.py:34
  78.7 0.1 reshape.45
  78.8 0.1 reshape.46
  78.9 8.0 %all_to_all.37 = bf16[8,2,512]{2,1,0:T(2,128)(2,1)S(1)} all-to-all(bf16[8,2,512]{2,1,0:T(2,128)(2,1)S(1)} %reshape.46), channel_id=1, replica_groups=mesh['tp'=8,'row'=8,'col'=8] {'col'}, dimensions={0} | all-to-all | bytes 32768 | tf_op jit(solution)/shard_map/all_to_all | solution.py:11
  86.9 0.0 copy-done.2
  86.9 1.3 broadcast_in_dim.10
  88.2 8.8 %all-to-all-start.3 = ((bf16[64,64,128]{2,1,0:T(8,128)(2,1)}), bf16[64,64,128]{2,1,0:T(8,128)(2,1)S(1)}, u32[]{:S(2)}, u32[]{:S(2)}) async-start(bf16[64,64,128]{2,1,0:T(8,128)(2,1)} %broadcast_in_dim.10), calls=%async_computation.3 | async-start | bytes 2097152 | tf_op jit(solution)/shard_map/all_to_all | solution.py:11
  97.0 0.0 all-gather.2.cloned.1.call-start
  97.0 0.7 all-gather.2.cloned.1.call-update
  97.7 0.1 reshape.47
  97.8 30.5 %all-to-all-done.3 = bf16[64,64,128]{2,1,0:T(8,128)(2,1)S(1)} async-done(((bf16[64,64,128]{2,1,0:T(8,128)(2,1)}), bf16[64,64,128]{2,1,0:T(8,128)(2,1)S(1)}, u32[]{:S(2)}, u32[]{:S(2)}) %all-to-all-start.3) | async-done | bytes 1048608 | tf_op jit(solution)/shard_map/all_to_all | solution.py:11
  128.3 104.7 %all-gather.2.cloned.1.call-done = bf16[128,4096]{0,1:T(8,128)(2,1)} async-done(((bf16[128,64]{0,1:T(8,128)(2,1)}), bf16[128,4096]{0,1:T(8,128)(2,1)}) %all-gather.2.cloned.1.call-update) | async-done | bytes 1048592 | tf_op jit(solution)/shard_map/all_gather | solution.py:59
  233.1 0.0 copy-done.1
  233.1 1.8 fusion.4
  234.9 1.1 fusion
  236.0 0.1 copy.18
  236.1 0.7 reshape.48
  236.8 18.4 %all_to_all.38 = bf16[8,2,16384]{2,1,0:T(2,128)(2,1)} all-to-all(bf16[8,2,16384]{2,1,0:T(2,128)(2,1)S(1)} %reshape.48), channel_id=1, replica_groups=mesh['tp'=8,'row'=8,'col'=8] {'col'}, dimensions={0} | all-to-all | bytes 1048576 | tf_op jit(solution)/shard_map/all_to_all | solution.py:34
  255.3 2.3 reshape.49
  257.6 0.2 bitcast_reduce_fusion
  257.8 0.1 copy.12
  257.9 0.1 convert_element_type.33
  258.1 20.5 %all_to_all.39 = bf16[8,64,512]{2,1,0:T(8,128)(2,1)S(1)} all-to-all(bf16[8,64,512]{2,1,0:T(8,128)(2,1)S(1)} %broadcast_in_dim.11), channel_id=1, replica_groups=mesh['tp'=8,'row'=8,'col'=8] {'row'}, dimensions={0} | all-to-all | bytes 1048576 | tf_op jit(solution)/shard_map/all_to_all | solution.py:11
  278.5 1.2 convolution_convert_fusion
  279.7 47.1 %all_to_all.40 = bf16[8,64,1792]{2,1,0:T(8,128)(2,1)S(1)} all-to-all(bf16[8,64,1792]{2,1,0:T(8,128)(2,1)S(1)} %bitcast.36), channel_id=1, replica_groups=mesh['tp'=8,'row'=8,'col'=8] {'tp'}, dimensions={0} | all-to-all | bytes 3670016 | tf_op jit(solution)/shard_map/all_to_all | solution.py:34
  326.9 1.0 convert_reduce_fusion
  (4 shorter events, 0.1 us)
Async XLA Ops:
  6.5 51.6 %copy-start = (bf16[16,1792]{1,0:T(8,128)(2,1)S(1)}, bf16[16,1792]{1,0:T(8,128)(2,1)}, u32[]{:S(2)}) copy-start(bf16[16,1792]{1,0:T(8,128)(2,1)} %param.5) | copy-start | bytes 172036
  58.1 28.8 %copy-start.2 = (bf16[64,128]{1,0:T(8,128)(2,1)S(1)}, bf16[64,128]{1,0:T(8,128)(2,1)}, u32[]{:S(2)}) copy-start(bf16[64,128]{1,0:T(8,128)(2,1)} %param.8) | copy-start | bytes 49156
  58.5 174.6 %copy-start.1 = (f32[64,128]{1,0:T(8,128)S(1)}, f32[64,128]{1,0:T(8,128)}, u32[]{:S(2)}) copy-start(f32[64,128]{1,0:T(8,128)} %param.9) | copy-start | bytes 98308
  88.2 40.1 %all-to-all-start.3 = ((bf16[64,64,128]{2,1,0:T(8,128)(2,1)}), bf16[64,64,128]{2,1,0:T(8,128)(2,1)S(1)}, u32[]{:S(2)}, u32[]{:S(2)}) async-start(bf16[64,64,128]{2,1,0:T(8,128)(2,1)} %broadcast_in_dim.10), calls=%async_computation.3 | async-start | bytes 2097152 | tf_op jit(solution)/shard_map/all_to_all | solution.py:11
  97.0 136.1 %all-gather.2.cloned.1.call-start = ((), (), s32[]{:S(2)}) async-start(), calls=%async_computation.7 | async-start | bytes 1064960 | tf_op jit(solution)/shard_map/all_gather | solution.py:59
Sparse Core Ops, SparseCore 0:
  102.1 130.8 all-gather.1
where the time goes:
time: 335 us
  blocking collectives  165 us (49%)
  waiting for transfers between devices  136 us (41%)
  between operations  13.5 us (4%)
  starting transfers between devices  8.8 us (3%)
  local copies, waits for them, and re-layouts  6.28 us (2%)
  matrix products  4.45 us (1%)
    all_gather x1, waiting for transfers between devices, shards(): grad_full = lax.all_gather(out_grad, ('tp', 'row'), axis=1, tiled=True)  105 us
    all_to_all x3, blocking collectives, sent_and_summed(): lax.all_to_all(tiles, axis, split_axis=0, concat_axis=0, tiled=True)  85.5 us
    all_to_all x3, blocking collectives, sent_to_all(): lax.all_to_all(jnp.broadcast_to(array[None], (devices, *array.shape)), ax...  79 us
    all_to_all x1, waiting for transfers between devices, sent_to_all(): lax.all_to_all(jnp.broadcast_to(array[None], (devices, *array.shape)), ax...  30.5 us
    all_to_all x1, starting transfers between devices, sent_to_all(): lax.all_to_all(jnp.broadcast_to(array[None], (devices, *array.shape)), ax...  8.75 us
  transfers between devices with their start and end apart: 2, of which 2 were waited for; matrix products, arithmetic and copies ran while one was open for 0% of the time, Pallas kernels for 0%

commit v1 on v0

--- a/solution.py
+++ b/solution.py
@@ -56,7 +56,10 @@
     rotated_in = gathered_copies(rotated_in, "col", 0)
     queries = rotated_in.shape[0]
     out_rows = gathered_copies(basis_out, ("tp", "row"), 0)
-    grad_full = lax.all_gather(out_grad, ("tp", "row"), axis=1, tiled=True)
+    grad_full = jnp.concatenate(
+        lax.all_to_all(jnp.stack([out_grad] * lax.axis_size(("tp", "row"))), ("tp", "row"), 0, 0),
+        axis=1,
+    )
     rotated_out = jnp.dot(grad_full, out_rows, preferred_element_type=jnp.float32).astype(
         jnp.bfloat16
     )

time: 335 us -> 256 us (0.76)
  waiting for transfers between devices: 136 us -> 60.9 us
  between operations: 13.5 us -> 0.12 us
  starting transfers between devices: 8.8 us -> 16.4 us
    all_gather x1 -> x0, waiting for transfers between devices: 105 us -> none  [shards(): grad_full = lax.all_gather(out_grad, ('tp', 'row'), axis=1, tiled=True)]
    all_to_all x0 -> x1, waiting for transfers between devices: none -> 31.2 us  [shards(): lax.all_to_all(jnp.stack([out_grad] * lax.axis_size(('tp', 'row'))), ('tp...]
    all_to_all x0 -> x1, starting transfers between devices: none -> 7.62 us  [shards(): lax.all_to_all(jnp.stack([out_grad] * lax.axis_size(('tp', 'row'))), ('tp...]
where the time goes in v1:
time: 256 us; the launch traced here: 255 us
  blocking collectives  164 us (64%)
  waiting for transfers between devices  60.9 us (24%)
  starting transfers between devices  16.4 us (6%)
  local copies, waits for them, and re-layouts  7.53 us (3%)
  matrix products  4.45 us (2%)
    all_to_all x3, blocking collectives, sent_and_summed(): lax.all_to_all(tiles, axis, split_axis=0, concat_axis=0, tiled=True)  84.3 us
    all_to_all x3, blocking collectives, sent_to_all(): lax.all_to_all(jnp.broadcast_to(array[None], (devices, *array.shape)), ax...  80.1 us
    all_to_all x1, waiting for transfers between devices, shards(): lax.all_to_all(jnp.stack([out_grad] * lax.axis_size(('tp', 'row'))), ('tp...  31.2 us
    all_to_all x1, waiting for transfers between devices, sent_to_all(): lax.all_to_all(jnp.broadcast_to(array[None], (devices, *array.shape)), ax...  29.7 us
    all_to_all x1, starting transfers between devices, sent_to_all(): lax.all_to_all(jnp.broadcast_to(array[None], (devices, *array.shape)), ax...  8.75 us
    all_to_all x1, starting transfers between devices, shards(): lax.all_to_all(jnp.stack([out_grad] * lax.axis_size(('tp', 'row'))), ('tp...  7.62 us
  transfers between devices with their start and end apart: 2, of which 2 were waited for; matrix products, arithmetic and copies ran while one was open for 0% of the time, Pallas kernels for 0%

profile of v1, /device:TPU:8, one launch (start us, length us, event | category | flops | bytes accessed | tf_op | source)
XLA Modules:
  0.0 255.0 jit_solution(4505531096859930628)
XLA Ops:
  0.0 0.0 copy-start
  0.0 1.1 broadcast_in_dim.8
  1.1 50.5 %all_to_all.40 = bf16[8,224,512]{2,1,0:T(8,128)(2,1)S(1)} all-to-all(bf16[8,224,512]{2,1,0:T(8,128)(2,1)S(1)} %broadcast_in_dim.8), channel_id=1, replica_groups=mesh['tp'=8,'row'=8,'col'=8] {'col'}, dimensions={0} | all-to-all | bytes 3670016 | tf_op jit(solution)/shard_map/all_to_all | solution.py:11
  51.6 0.0 copy-start.1
  51.6 0.0 copy-done
  51.6 0.3 convolution_convert_fusion.2
  51.9 0.0 copy-start.2
  51.9 0.1 reshape.41
  52.1 0.1 reshape.49
  52.2 20.0 %all_to_all.41 = bf16[8,2,512]{2,1,0:T(2,128)(2,1)S(1)} all-to-all(bf16[8,2,512]{2,1,0:T(2,128)(2,1)S(1)} %reshape.49), channel_id=1, replica_groups=mesh['tp'=8,'row'=8,'col'=8] {'row'}, dimensions={0} | all-to-all | bytes 32768 | tf_op jit(solution)/shard_map/all_to_all | solution.py:34
  72.1 0.0 copy-done.1
  72.1 1.2 broadcast_in_dim.10
  73.4 8.8 %all-to-all-start.4 = ((bf16[64,64,128]{2,1,0:T(8,128)(2,1)}), bf16[64,64,128]{2,1,0:T(8,128)(2,1)S(1)}, u32[]{:S(2)}, u32[]{:S(2)}) async-start(bf16[64,64,128]{2,1,0:T(8,128)(2,1)} %broadcast_in_dim.10), calls=%async_computation.4 | async-start | bytes 2097152 | tf_op jit(solution)/shard_map/all_to_all | solution.py:11
  82.1 0.0 copy-start.3
  82.1 0.1 reshape.50
  82.3 0.1 reshape.51
  82.4 29.7 %all-to-all-done.4 = bf16[64,64,128]{2,1,0:T(8,128)(2,1)S(1)} async-done(((bf16[64,64,128]{2,1,0:T(8,128)(2,1)}), bf16[64,64,128]{2,1,0:T(8,128)(2,1)S(1)}, u32[]{:S(2)}, u32[]{:S(2)}) %all-to-all-start.4) | async-done | bytes 1048608 | tf_op jit(solution)/shard_map/all_to_all | solution.py:11
  112.1 8.4 %all_to_all.42 = bf16[8,2,512]{2,1,0:T(2,128)(2,1)S(1)} all-to-all(bf16[8,2,512]{2,1,0:T(2,128)(2,1)S(1)} %reshape.51), channel_id=1, replica_groups=mesh['tp'=8,'row'=8,'col'=8] {'col'}, dimensions={0} | all-to-all | bytes 32768 | tf_op jit(solution)/shard_map/all_to_all | solution.py:11
  120.5 0.0 copy-done.2
  120.5 1.3 stack.2
  121.8 7.6 %all-to-all-start.3 = ((bf16[64,128,64]{1,2,0:T(8,128)(2,1)}), bf16[64,128,64]{1,2,0:T(8,128)(2,1)}, u32[]{:S(2)}, u32[]{:S(2)}) async-start(bf16[64,128,64]{1,2,0:T(8,128)(2,1)} %stack.2), calls=%async_computation.3 | async-start | bytes 2097152 | tf_op jit(solution)/shard_map/all_to_all | solution.py:60
  129.4 0.1 reshape.52
  129.5 31.2 %all-to-all-done.3 = bf16[64,128,64]{1,2,0:T(8,128)(2,1)} async-done(((bf16[64,128,64]{1,2,0:T(8,128)(2,1)}), bf16[64,128,64]{1,2,0:T(8,128)(2,1)}, u32[]{:S(2)}, u32[]{:S(2)}) %all-to-all-start.3) | async-done | bytes 1048608 | tf_op jit(solution)/shard_map/all_to_all | solution.py:60
  160.7 0.0 copy-done.3
  160.7 1.8 fusion.5
  162.5 1.1 fusion
  163.6 0.1 copy.19
  163.7 0.7 reshape.53
  164.5 18.4 %all_to_all.43 = bf16[8,2,16384]{2,1,0:T(2,128)(2,1)} all-to-all(bf16[8,2,16384]{2,1,0:T(2,128)(2,1)S(1)} %reshape.53), channel_id=1, replica_groups=mesh['tp'=8,'row'=8,'col'=8] {'col'}, dimensions={0} | all-to-all | bytes 1048576 | tf_op jit(solution)/shard_map/all_to_all | solution.py:34
  182.9 2.3 reshape.54
  185.2 0.2 bitcast_reduce_fusion
  185.4 0.1 copy.13
  185.5 0.1 convert_element_type.33
  185.7 21.2 %all_to_all.44 = bf16[8,64,512]{2,1,0:T(8,128)(2,1)S(1)} all-to-all(bf16[8,64,512]{2,1,0:T(8,128)(2,1)S(1)} %broadcast_in_dim.11), channel_id=1, replica_groups=mesh['tp'=8,'row'=8,'col'=8] {'row'}, dimensions={0} | all-to-all | bytes 1048576 | tf_op jit(solution)/shard_map/all_to_all | solution.py:11
  206.9 1.2 convolution_convert_fusion
  208.1 45.9 %all_to_all.45 = bf16[8,64,1792]{2,1,0:T(8,128)(2,1)S(1)} all-to-all(bf16[8,64,1792]{2,1,0:T(8,128)(2,1)S(1)} %bitcast.49), channel_id=1, replica_groups=mesh['tp'=8,'row'=8,'col'=8] {'tp'}, dimensions={0} | all-to-all | bytes 3670016 | tf_op jit(solution)/shard_map/all_to_all | solution.py:34
  254.0 1.0 convert_reduce_fusion
  (4 shorter events, 0.1 us)
Async XLA Ops:
  0.0 51.6 %copy-start = (bf16[16,1792]{1,0:T(8,128)(2,1)S(1)}, bf16[16,1792]{1,0:T(8,128)(2,1)}, u32[]{:S(2)}) copy-start(bf16[16,1792]{1,0:T(8,128)(2,1)} %param.5) | copy-start | bytes 172036
  51.6 20.5 %copy-start.1 = (bf16[64,128]{1,0:T(8,128)(2,1)S(1)}, bf16[64,128]{1,0:T(8,128)(2,1)}, u32[]{:S(2)}) copy-start(bf16[64,128]{1,0:T(8,128)(2,1)} %param.8) | copy-start | bytes 49156
  51.9 68.5 %copy-start.2 = (bf16[128,64]{0,1:T(8,128)(2,1)S(1)}, bf16[128,64]{0,1:T(8,128)(2,1)}, u32[]{:S(2)}) copy-start(bf16[128,64]{0,1:T(8,128)(2,1)} %param.6) | copy-start | bytes 49156
  73.4 38.7 %all-to-all-start.4 = ((bf16[64,64,128]{2,1,0:T(8,128)(2,1)}), bf16[64,64,128]{2,1,0:T(8,128)(2,1)S(1)}, u32[]{:S(2)}, u32[]{:S(2)}) async-start(bf16[64,64,128]{2,1,0:T(8,128)(2,1)} %broadcast_in_dim.10), calls=%async_computation.4 | async-start | bytes 2097152 | tf_op jit(solution)/shard_map/all_to_all | solution.py:11
  82.1 78.5 %copy-start.3 = (f32[64,128]{1,0:T(8,128)S(1)}, f32[64,128]{1,0:T(8,128)}, u32[]{:S(2)}) copy-start(f32[64,128]{1,0:T(8,128)} %param.9) | copy-start | bytes 98308
  121.8 38.9 %all-to-all-start.3 = ((bf16[64,128,64]{1,2,0:T(8,128)(2,1)}), bf16[64,128,64]{1,2,0:T(8,128)(2,1)}, u32[]{:S(2)}, u32[]{:S(2)}) async-start(bf16[64,128,64]{1,2,0:T(8,128)(2,1)} %stack.2), calls=%async_computation.3 | async-start | bytes 2097152 | tf_op jit(solution)/shard_map/all_to_all | solution.py:60
